TPU v7x, 256 devices: a 8x8x2 block of a 8x8x16 slice. The times are simulated.
256 devices in a mesh: rep: 2 (over z), exp: 128 (over x, y, core).
Axes of the slice: x: 8, y: 8, z: 2, core: 2. Of those that a mesh axis runs over, the one named last changes fastest.
The devices are a block of a 8x8x16 slice.
Arguments:
- a_tokens: bfloat16 [512, 7168], P(('rep', 'exp')), parts along dimension 0, may hold values from -6 to 6
- a_gain: float32 [7168], replicated, may hold values from 0.25 to 1.75
- dense_gate: bfloat16 [7168, 18432], P(None, 'exp'), may hold values from -0.0625 to 0.0625
- dense_up: bfloat16 [7168, 18432], P(None, 'exp'), may hold values from -0.0625 to 0.0625
- dense_down: bfloat16 [18432, 7168], P('exp'), may hold values from -0.046875 to 0.046875
- b_tokens: bfloat16 [1024, 7168], P(('rep', 'exp')), parts along dimension 0, may hold values from -6 to 6
- b_gain: float32 [7168], replicated, may hold values from 0.25 to 1.75
- expert_ids: int32 [1024, 8], P(('rep', 'exp')), parts along dimension 0, may hold values from 0 to 15, all different within a row; in each aligned block of 4 rows (0 to 3, 4 to 7, ...) at most 3 rows name the same one
- route_weights: float32 [1024, 8], P(('rep', 'exp')), parts along dimension 0, may hold values from 0.05 to 0.5
- expert_gate: bfloat16 [128, 7168, 128], P('exp'), may hold values from -0.0625 to 0.0625
- expert_up: bfloat16 [128, 7168, 128], P('exp'), may hold values from -0.0625 to 0.0625
- expert_down: bfloat16 [128, 128, 7168], P('exp'), may hold values from -0.1875 to 0.1875
Outputs:
- a_out: bfloat16 [512, 7168], P(('rep', 'exp')), parts along dimension 0
- b_out: bfloat16 [1024, 7168], P(('rep', 'exp')), parts along dimension 0
There are 2 independent parts, one for each index of `rep`. A program takes and returns all parts, laid end to end along the dimension named above; an argument that names none is the same for every part. Nothing has to cross between parts.
Inputs may be any that keep to these rules, and one draw needn't show every extreme that they name: `expert_ids`: each row names 8 different experts. Among the rows of one device no expert is named more than 3 times, and in some devices one expert is named exactly 3 times.
All inputs are finite; a program needn't handle non-finite values.
Results may differ from a plain program's by a relative error of at most 0.008.
Values may be sent and summed in bfloat16 or wider, within the bound.
A program may use at most 128 MiB of HBM per device.

v0:
```python
import jax
import jax.numpy as jnp
from jax import lax
from jax.sharding import Mesh
from jax.sharding import PartitionSpec as P

EXPERTS = 16
CAP = 3
EXP = ("exp_0", "exp_1", "exp_2")
REP_EXP = ("rep", "exp_0", "exp_1", "exp_2")


def cut_along(array, dim, devices):
    before, after = (array.shape[:dim], array.shape[dim + 1 :])
    return jnp.moveaxis(array.reshape(*before, devices, -1, *after), dim, 0)


def scatter_lines(array, axis, dim):
    devices = lax.axis_size(axis)
    blocks = cut_along(array, dim, devices)
    lines = blocks.reshape(devices, -1)
    rows = max(16, -(-lines.shape[1] // 1024) * 8)
    lines = jnp.pad(lines, ((0, 0), (0, rows * 128 - lines.shape[1]))).reshape(-1, 128)
    own = lax.psum_scatter(lines, axis, scatter_dimension=0, tiled=True)
    return own.reshape(-1)[: blocks[0].size].reshape(blocks.shape[1:])


def joined_along(blocks, dim):
    lengths = list(blocks.shape[1:])
    lengths[dim] *= blocks.shape[0]
    return jnp.moveaxis(blocks, 0, dim).reshape(lengths)


def exchange_in_order(blocks, axes, sequence):
    lengths = [lax.axis_size(a) for a in axes]
    blocks = blocks.reshape(*lengths, *blocks.shape[1:])
    for k in sequence:
        blocks = lax.all_to_all(blocks, axes[k], split_axis=k, concat_axis=k, tiled=True)
    return blocks.reshape(-1, *blocks.shape[len(axes) :])


def two_step_exchange(array, groups, sequence, split_dim, concat_dim):
    devices = lax.axis_size(groups[0]) * lax.axis_size(groups[1])
    blocks = cut_along(array, split_dim, devices)
    return joined_along(exchange_in_order(blocks, groups, sequence), concat_dim)


def from_partner(array, axis, distance):
    return lax.ppermute(array, axis, [(i, i ^ 1 << distance) for i in range(lax.axis_size(axis))])


def normed(values, gain_vec):
    return values * lax.rsqrt(jnp.mean(values * values, axis=-1, keepdims=True) + 1e-06) * gain_vec


def shards(
    a_tokens,
    a_gain,
    dense_gate,
    dense_up,
    dense_down,
    b_tokens,
    b_gain,
    expert_ids,
    route_weights,
    expert_gate,
    expert_up,
    expert_down,
):
    devices = lax.axis_size(EXP)
    group_size = devices // EXPERTS
    model_width = b_tokens.shape[1]
    a_float = a_tokens.astype(jnp.float32)
    a_normed = normed(a_float, a_gain).astype(jnp.bfloat16)
    block_rows = lax.all_gather(a_normed, EXP, axis=0, tiled=True)
    gate_proj = jnp.dot(block_rows, dense_gate, preferred_element_type=jnp.float32)
    up_proj = jnp.dot(block_rows, dense_up, preferred_element_type=jnp.float32)
    hidden = (jax.nn.silu(gate_proj) * up_proj).astype(jnp.bfloat16)
    block_rows = hidden
    a_sum = scatter_lines(
        jnp.dot(block_rows, dense_down, preferred_element_type=jnp.float32), EXP, 0
    )
    a_out = (a_float + a_sum).astype(jnp.bfloat16)
    row_count = b_tokens.shape[0]
    b_float = b_tokens.astype(jnp.float32)
    b_normed = normed(b_float, b_gain).astype(jnp.bfloat16)
    onehot = (expert_ids[:, :, None] == jnp.arange(EXPERTS, dtype=jnp.int32)[None, None, :]).astype(
        jnp.float32
    )
    chosen = jnp.sum(onehot, axis=1)
    before = jnp.cumsum(chosen, axis=0) - chosen
    slot_hit = (before[:, :, None] == jnp.arange(CAP, dtype=jnp.float32)[None, None, :]).astype(
        jnp.float32
    ) * chosen[:, :, None]
    weights_te = jnp.einsum("tk,tke->te", route_weights, onehot)
    placing = slot_hit.reshape(row_count, EXPERTS * CAP)
    mixing = (weights_te[:, :, None] * slot_hit).reshape(row_count, EXPERTS * CAP)
    packed = jnp.dot(placing.T.astype(jnp.bfloat16), b_normed, preferred_element_type=jnp.float32)
    packed = packed.astype(jnp.bfloat16).reshape(EXPERTS, CAP, model_width)
    w_gate = expert_gate[0]
    w_up = expert_up[0]
    w_down = expert_down[0]
    narrow = model_width // group_size
    outgoing = (
        packed.reshape(EXPERTS, CAP, group_size, narrow)
        .transpose(0, 2, 1, 3)
        .reshape(devices, CAP, narrow)
    )
    arrived = two_step_exchange(outgoing, (("exp_0", "exp_1"), "exp_2"), (1, 0), 0, 0)
    position = lax.axis_index(EXP) % group_size
    for bit_number in range(group_size.bit_length() - 1):
        partner = from_partner(arrived, EXP, bit_number)
        high_bit = position >> bit_number & 1 == 1
        arrived = jnp.where(
            high_bit, jnp.concatenate([partner, arrived], 2), jnp.concatenate([arrived, partner], 2)
        )
    sources = arrived.shape[0]
    item_count = arrived.shape[1]
    flat_rows = arrived.reshape(sources * item_count, model_width)
    gate_proj = jnp.dot(flat_rows, w_gate, preferred_element_type=jnp.float32)
    up_proj = jnp.dot(flat_rows, w_up, preferred_element_type=jnp.float32)
    hid_rows = (jax.nn.silu(gate_proj) * up_proj).astype(jnp.bfloat16)
    partial_value = jnp.dot(hid_rows, w_down, preferred_element_type=jnp.float32).astype(
        jnp.bfloat16
    )
    partial_value = partial_value.reshape(sources, item_count, model_width)
    returned = lax.all_to_all(partial_value, EXP, split_axis=0, concat_axis=0, tiled=True)
    expert_out = jnp.sum(
        returned.reshape(EXPERTS, group_size, CAP, model_width).astype(jnp.float32), axis=1
    )
    expert_out = expert_out.astype(jnp.bfloat16).reshape(EXPERTS * CAP, model_width)
    b_sum = jnp.dot(mixing, expert_out.astype(jnp.float32))
    b_out = (b_float + b_sum).astype(jnp.bfloat16)
    return (a_out, b_out)


def solution(mesh):
    finer = Mesh(
        mesh.devices.reshape(mesh.shape["rep"], 8, 8, 2), ("rep", "exp_0", "exp_1", "exp_2")
    )
    placed = (
        P(REP_EXP, None),
        P(),
        P(None, EXP),
        P(None, EXP),
        P(EXP, None),
        P(REP_EXP, None),
        P(),
        P(REP_EXP, None),
        P(REP_EXP, None),
        P(EXP, None, None),
        P(EXP, None, None),
        P(EXP, None, None),
    )
    return jax.shard_map(
        shards,
        mesh=finer,
        in_specs=placed,
        out_specs=(P(REP_EXP, None), P(REP_EXP, None)),
        check_vma=False,
    )
```

profile of v0, /device:TPU:513, one launch (start us, length us, event | category | flops | bytes accessed | tf_op | source)
XLA Modules:
  0.0 552.7 jit_solution(1277991353424163101)
XLA Ops:
  11.4 24.3 %all_to_all.15 = bf16[64,2,1,3,896]{4,0,3,2,1:T(8,128)(2,1)S(1)} all-to-all(bf16[64,2,1,3,896]{4,0,3,2,1:T(8,128)(2,1)S(1)} %copy.40), channel_id=1, replica_groups=mesh['rep'=2,'exp_0'=8,'exp_1'=8,'exp_2'=2] {'exp_2'}, dimensions={1} | all-to-all | bytes 1376256 | tf_op jit(solution)/shard_map/all_to_all | solution.py:38
  37.3 6.5 %all-to-all-start.1 = ((bf16[64,2,1,3,896]{4,1,3,2,0:T(2,128)(2,1)}), bf16[64,2,1,3,896]{4,1,3,2,0:T(2,128)(2,1)S(1)}, u32[]{:S(2)}, u32[]{:S(2)}) async-start(bf16[64,2,1,3,896]{4,1,3,2,0:T(2,128)(2,1)} %copy.41), calls=%async_computation.2 | async-start | bytes 1376256 | tf_op jit(solution)/shard_map/all_to_all | solution.py:38
  44.1 18.9 %all-to-all-done.1 = bf16[64,2,1,3,896]{4,1,3,2,0:T(2,128)(2,1)S(1)} async-done(((bf16[64,2,1,3,896]{4,1,3,2,0:T(2,128)(2,1)}), bf16[64,2,1,3,896]{4,1,3,2,0:T(2,128)(2,1)S(1)}, u32[]{:S(2)}, u32[]{:S(2)}) %all-to-all-start.1) | async-done | bytes 688160 | tf_op jit(solution)/shard_map/all_to_all | solution.py:38
  68.8 3.0 maximum_select_fusion.3
  72.2 32.3 %collective-permute-done.1 = bf16[128,3,1792]{2,0,1:T(8,128)(2,1)} collective-permute-done((bf16[128,3,1792]{2,0,1:T(8,128)(2,1)}, bf16[128,3,1792]{2,0,1:T(8,128)(2,1)}, u32[]{:S(2)}, u32[]{:S(2)}) %collective-permute-start.1) | collective-permute-done | bytes 1376288 | tf_op jit(solution)/shard_map/ppermute | solution.py:49
  104.5 4.3 maximum_select_fusion.1
  112.1 3.0 concatenate.47
  120.3 3.8 copy.44
  124.0 4.2 concatenate.45
  128.2 3.7 maximum_select_fusion.2
  131.9 106.7 %collective-permute-done.2 = bf16[128,3,3584]{2,0,1:T(8,128)(2,1)} collective-permute-done((bf16[128,3,3584]{2,0,1:T(8,128)(2,1)}, bf16[128,3,3584]{2,0,1:T(8,128)(2,1)}, u32[]{:S(2)}, u32[]{:S(2)}) %collective-permute-start.2) | collective-permute-done | bytes 2752544 | tf_op jit(solution)/shard_map/ppermute | solution.py:49
  238.6 5.9 %copy.43 = bf16[128,3,3584]{2,1,0:T(4,128)(2,1)} copy(bf16[128,3,3584]{2,0,1:T(8,128)(2,1)} %collective-permute-done.2) | data formatting | bytes 5505024 | tf_op jit(solution)/shard_map/ppermute | solution.py:49
  244.5 7.0 %concatenate.44 = bf16[384,3584]{1,0:T(8,128)(2,1)} reshape(bf16[128,3,3584]{2,1,0:T(4,128)(2,1)} %copy.43) | data formatting | bytes 5505024 | tf_op jit(solution)/shard_map/concatenate | solution.py:115
  251.6 6.4 %fusion.3 = f32[384,128]{1,0:T(8,128)S(1)} fusion(bf16[1,7168,128]{2,1,0:T(8,128)(2,1)} %param.22, bf16[384,3584]{1,0:T(8,128)(2,1)} %maximum_select_fusion.2, bf16[384,3584]{1,0:T(8,128)(2,1)} %concatenate.44, pred[]{:T(512)S(6)} %eq.54), kind=kOutput, calls=%fused_computation.10 | convolution fusion | flops 729415680 | bytes 7536641 | tf_op jit(solution)/shard_map/dot_general | solution.py:121
  258.0 9.6 %convolution_convert_fusion = bf16[384,7168]{1,0:T(8,128)(2,1)} fusion(bf16[1,128,7168]{2,1,0:T(8,128)(2,1)} %param.23, f32[384,128]{1,0:T(8,128)S(1)} %fusion.3, bf16[1,7168,128]{2,1,0:T(8,128)(2,1)} %param.21, bf16[384,3584]{1,0:T(8,128)(2,1)} %maximum_select_fusion.2, bf16[384,3584]{1,0:T(8,128)(2,1)} %concatenate.44, pred[]{:T(512)S(6)} %eq.54), kind=kOutput, calls=%fused_computation | convolution fusion | flops 1437106176 | bytes 14876673 | tf_op jit(solution)/shard_map/dot_general | solution.py:123
  267.6 12.3 %reshape.66 = bf16[128,3,7168]{2,1,0:T(4,128)(2,1)} reshape(bf16[384,7168]{1,0:T(8,128)(2,1)} %convolution_convert_fusion) | data formatting | bytes 11010048 | tf_op jit(solution)/shard_map/reshape | solution.py:126
  279.9 9.5 %all-to-all-start.2 = ((bf16[128,3,7168]{2,1,0:T(4,128)(2,1)}), bf16[128,3,7168]{2,1,0:T(4,128)(2,1)}, u32[]{:S(2)}, u32[]{:S(2)}) async-start(bf16[128,3,7168]{2,1,0:T(4,128)(2,1)} %reshape.66), calls=%async_computation.3 | async-start | bytes 14680064 | tf_op jit(solution)/shard_map/all_to_all | solution.py:127
  289.6 8.4 %reshape.69 = bf16[256,7168]{1,0:T(8,128)(2,1)} reshape(bf16[128,2,7168]{2,1,0:T(2,128)(2,1)} %all-gather.3.cloned.1.call-done) | data formatting | bytes 7340032
  297.9 4.1 fusion.42
  302.0 9.9 %fusion.8 = f32[256,7168]{1,0:T(8,128)} fusion(bf16[144,7168]{1,0:T(8,128)(2,1)S(1)} %copy-done, bf16[256,7168]{1,0:T(8,128)(2,1)} %reshape.69, bf16[7168,144]{0,1:T(8,128)(2,1)} %param.15, f32[256,144]{0,1:T(8,128)S(1)} %fusion.42), kind=kOutput, calls=%fused_computation.18 | convolution fusion | flops 1057185792 | bytes 15286272 | tf_op jit(solution)/shard_map/dot_general | solution.py:81
  311.9 8.4 %reshape.65 = f32[14336,128]{1,0:T(8,128)} reshape(f32[256,7168]{1,0:T(8,128)} %fusion.8) | data formatting | bytes 14680064 | tf_op jit(solution)/shard_map/reshape | solution.py:23
  321.3 151.8 %all-to-all-done.2 = bf16[128,3,7168]{2,1,0:T(4,128)(2,1)} async-done(((bf16[128,3,7168]{2,1,0:T(4,128)(2,1)}), bf16[128,3,7168]{2,1,0:T(4,128)(2,1)}, u32[]{:S(2)}, u32[]{:S(2)}) %all-to-all-start.2) | async-done | bytes 5505056 | tf_op jit(solution)/shard_map/all_to_all | solution.py:127
  473.2 6.8 %bitcast_reduce_fusion = bf16[16,3,7168]{2,1,0:T(4,128)(2,1)S(1)} fusion(bf16[128,3,7168]{2,1,0:T(4,128)(2,1)} %all-to-all-done.2), kind=kLoop, calls=%fused_computation.5 | loop fusion | flops 2408448 | bytes 6193152 | tf_op jit(solution)/shard_map/reduce_sum | solution.py:128
  481.0 63.3 %reduce-scatter.2.cloned.1.call-done = f32[112,128]{1,0:T(8,128)} async-done(((f32[14336,128]{1,0:T(8,128)}), f32[112,128]{1,0:T(8,128)}) %reduce-scatter.2.cloned.1.call-update) | async-done | bytes 57360 | tf_op jit(solution)/shard_map/reduce_scatter | solution.py:24
  (55 shorter events, 24.3 us)
Async XLA Ops:
  7.2 294.8 %copy-start = (bf16[144,7168]{1,0:T(8,128)(2,1)S(1)}, bf16[144,7168]{1,0:T(8,128)(2,1)}, u32[]{:S(2)}) copy-start(bf16[144,7168]{1,0:T(8,128)(2,1)} %param.16) | copy-start | bytes 6193156
  11.3 32.6 %copy-start.2 = (bf16[2,7168]{1,0:T(2,128)(2,1)S(1)}, bf16[2,7168]{1,0:T(2,128)(2,1)}, u32[]{:S(2)}) copy-start(bf16[2,7168]{1,0:T(2,128)(2,1)} %param.12) | copy-start | bytes 86020
  35.7 31.1 %copy-start.4 = (f32[7168]{0:T(1024)S(1)}, f32[7168]{0:T(1024)}, u32[]{:S(2)}) copy-start(f32[7168]{0:T(1024)} %param.13) | copy-start | bytes 86020
  37.3 25.7 %all-to-all-start.1 = ((bf16[64,2,1,3,896]{4,1,3,2,0:T(2,128)(2,1)}), bf16[64,2,1,3,896]{4,1,3,2,0:T(2,128)(2,1)S(1)}, u32[]{:S(2)}, u32[]{:S(2)}) async-start(bf16[64,2,1,3,896]{4,1,3,2,0:T(2,128)(2,1)} %copy.41), calls=%async_computation.2 | async-start | bytes 1376256 | tf_op jit(solution)/shard_map/all_to_all | solution.py:38
  43.8 245.8 %all-gather.3.cloned.1.call-start = ((), (), s32[]{:S(2)}) async-start(), calls=%async_computation.5 | async-start | bytes 3698688 | tf_op jit(solution)/shard_map/all_gather | solution.py:75
  64.5 4.3 collective-permute-start
  68.8 40.0 %copy-start.1 = (bf16[128,3,896]{2,0,1:T(8,128)(2,1)}, bf16[128,3,896]{2,0,1:T(8,128)(2,1)S(1)}, u32[]{:S(2)}) copy-start(bf16[128,3,896]{2,0,1:T(8,128)(2,1)S(1)} %collective-permute-done) | copy-start | bytes 2064388
  71.8 32.7 %collective-permute-start.1 = (bf16[128,3,1792]{2,0,1:T(8,128)(2,1)}, bf16[128,3,1792]{2,0,1:T(8,128)(2,1)}, u32[]{:S(2)}, u32[]{:S(2)}) collective-permute-start(bf16[128,3,1792]{2,0,1:T(8,128)(2,1)} %maximum_select_fusion.3), channel_id=1, source_target_pairs={{0,2},{1,3},{2,0},{3,1},{4,6},{5,7},{6,4},{7,5},{8,10},{9,11},{10,... | collective-permute-start | bytes 4128776 | tf_op jit(solution)/shard_map/ppermute | solution.py:49
  108.8 129.8 %collective-permute-start.2 = (bf16[128,3,3584]{2,0,1:T(8,128)(2,1)}, bf16[128,3,3584]{2,0,1:T(8,128)(2,1)}, u32[]{:S(2)}, u32[]{:S(2)}) collective-permute-start(bf16[128,3,3584]{2,0,1:T(8,128)(2,1)} %maximum_select_fusion.1), channel_id=1, source_target_pairs={{0,4},{1,5},{2,6},{3,7},{4,0},{5,1},{6,2},{7,3},{8,12},{9,13},{10,... | collective-permute-start | bytes 8257544 | tf_op jit(solution)/shard_map/ppermute | solution.py:49
  279.9 193.3 %all-to-all-start.2 = ((bf16[128,3,7168]{2,1,0:T(4,128)(2,1)}), bf16[128,3,7168]{2,1,0:T(4,128)(2,1)}, u32[]{:S(2)}, u32[]{:S(2)}) async-start(bf16[128,3,7168]{2,1,0:T(4,128)(2,1)} %reshape.66), calls=%async_computation.3 | async-start | bytes 14680064 | tf_op jit(solution)/shard_map/all_to_all | solution.py:127
  289.5 254.9 %reduce-scatter.2.cloned.1.call-start = ((), (), s32[]{:S(2)}) async-start(), calls=%async_computation.4 | async-start | bytes 7397376 | tf_op jit(solution)/shard_map/reduce_scatter | solution.py:24
  320.2 0.7 copy-start.5
  320.2 0.7 copy-start.6
  321.3 158.7 %copy-start.3 = (bf16[4,7168]{1,0:T(4,128)(2,1)S(1)}, bf16[4,7168]{1,0:T(4,128)(2,1)}, u32[]{:S(2)}) copy-start(bf16[4,7168]{1,0:T(4,128)(2,1)} %param.17) | copy-start | bytes 172036
Sparse Core Ops, SparseCore 0:
  67.7 173.2 all-gather.2
  320.4 223.8 reduce-scatter.1
where the time goes:
time: 558 us; the launch traced here: 553 us
  waiting for transfers between devices  374 us (67%)
  local copies, waits for them, and re-layouts  63 us (11%)
  matrix products  32.4 us (6%)
  blocking collectives  24.3 us (4%)
  other arithmetic  23.6 us (4%)
  starting transfers between devices  20.8 us (4%)
  between operations  14.2 us (3%)
    all_to_all x1, waiting for transfers between devices, shards(): lax.all_to_all(partial_value, EXP, split_axis=0, concat_axis=0, tiled=True)  152 us
    ppermute x3, waiting for transfers between devices, from_partner(): lax.ppermute(array, axis, [(i, i ^ 1 << distance) for i in range(lax.axis...  140 us
    reduce_scatter x1, waiting for transfers between devices, scatter_lines(): own = lax.psum_scatter(lines, axis, scatter_dimension=0, tiled=True)  63.3 us
    all_to_all x1, blocking collectives, exchange_in_order(): lax.all_to_all(blocks, axes[k], split_axis=k, concat_axis=k, tiled=True)  24.3 us
    all_to_all x1, waiting for transfers between devices, exchange_in_order(): lax.all_to_all(blocks, axes[k], split_axis=k, concat_axis=k, tiled=True)  18.9 us
    concatenate x4, local copies, waits for them, and re-layouts, shards(): jnp.concatenate([partner, arrived], 2)  15.5 us
    select_n x4, other arithmetic, shards(): jnp.where(high_bit, jnp.concatenate([partner, arrived], 2), jnp.concatena...  13.2 us
    reshape x1, local copies, waits for them, and re-layouts, shards(): partial_value = partial_value.reshape(sources, item_count, model_width)  12.3 us
  transfers between devices with their start and end apart: 7, of which 6 were waited for; matrix products, arithmetic and copies ran while one was open for 20% of the time, Pallas kernels for 0%

commit v1 on v0

v1 whole, which is shorter than its diff:
```python
import functools

import jax
import jax.numpy as jnp
from jax import lax
from jax.experimental import pallas as pl
from jax.experimental.pallas import tpu as pltpu
from jax.sharding import Mesh
from jax.sharding import PartitionSpec as P

EXPERTS = 16
REP_EXP = ("rep", "exp_0", "exp_1", "exp_2")
EXP = ("exp_0", "exp_1", "exp_2")
LONG = ("exp_1", "exp_0")
SHORT = ("exp_0", "exp_1")
BF16 = jnp.bfloat16
F32 = jnp.float32
MESH = pl.DeviceIdType.MESH
UNIT = 16


def iota2(rows, columns):
    shape = (rows, columns)
    return lax.broadcasted_iota(jnp.int32, shape, 0), lax.broadcasted_iota(jnp.int32, shape, 1)


def ones_where(condition):
    return jnp.where(condition, 1.0, 0.0).astype(BF16)


def silu(values):
    return values / (1.0 + jnp.exp(-values))


def kernel(
    n, u_ref, wg_hbm, wu_hbm, wd_hbm, eg_hbm, eu_hbm, ed_hbm, out_ref,
    xu, xa, xb, wg, wu, wd, egu, ed, acc_a, acc_b, oa, ob, pa, pb, ra, rb, yu, zu,
    w_sem, s1, r1, sa, ra_sem, sb, rb_sem, spa, rpa, spb, rpb,
    ta, qa, tb, qb, tpa, qpa, tpb, qpb, s2, r2,
):
    depth = wg.shape[0]
    half = depth // 2
    quarter = depth // 4
    wide = xb.shape[-1]
    block = 2 * n
    core = lax.axis_index("exp_2")
    other = 1 - core
    place = [lax.axis_index(LONG[0]), lax.axis_index(LONG[1])]
    spot = [place[1], place[0]]
    expert = ((lax.axis_index("exp_0") * n + lax.axis_index("exp_1")) * 2 + core) // (
        2 * n * n // EXPERTS
    )

    def along(position, distance):
        return lax.rem(position + distance + n, n)

    weights = [
        pltpu.make_async_copy(wg_hbm, wg, w_sem.at[0]),
        pltpu.make_async_copy(wu_hbm, wu, w_sem.at[1]),
        pltpu.make_async_copy(wd_hbm, wd, w_sem.at[2]),
        pltpu.make_async_copy(eg_hbm, egu.at[:, pl.ds(0, eg_hbm.shape[1])], w_sem.at[3]),
        pltpu.make_async_copy(
            eu_hbm, egu.at[:, pl.ds(eg_hbm.shape[1], eu_hbm.shape[1])], w_sem.at[4]
        ),
        pltpu.make_async_copy(ed_hbm, ed, w_sem.at[5]),
    ]
    for copy in weights:
        copy.start()

    barrier = pltpu.get_barrier_semaphore()
    pl.semaphore_signal(barrier, inc=1, device_id={"exp_2": other}, device_id_type=MESH)
    for h in range(2):
        for k in range(1, n):
            pl.semaphore_signal(
                barrier, inc=1, device_id={SHORT[h]: along(spot[h], k)}, device_id_type=MESH
            )
    pl.semaphore_wait(barrier, 2 * (n - 1) + 1)

    first = []
    for k in sorted(range(1, n), key=lambda k: -min(k, n - k)):
        for h in range(2):
            copy = pltpu.make_async_remote_copy(
                src_ref=u_ref.at[h], dst_ref=xu.at[h, spot[h]],
                send_sem=s1.at[h, k], recv_sem=r1.at[h, k],
                device_id={SHORT[h]: along(spot[h], k)}, device_id_type=MESH,
            )
            copy.start()
            first.append(copy)
    for h in range(2):
        xu[h, spot[h]] = u_ref[h]
    for copy in first:
        copy.wait()

    gathered = ((xa, sa, ra_sem, spa, rpa), (xb, sb, rb_sem, spb, rpb))
    half_cut = ((pl.ds(0, quarter), pl.ds(quarter, half - quarter)),
                (pl.ds(0, half), pl.ds(half, wide - half)))

    def hop(which, h, d, t, origin):
        ref, send, recv = gathered[which][:3]
        view = ref.at[h, core, origin]
        if t == n // 2:
            view = ref.at[h, core, origin, :, half_cut[which][d]]
        return pltpu.make_async_remote_copy(
            src_ref=view, dst_ref=view, send_sem=send.at[h, d, t - 1], recv_sem=recv.at[h, d, t - 1],
            device_id={LONG[h]: along(place[h], 1 - 2 * d)}, device_id_type=MESH,
        )

    def share(which, h, slot_core, origin, k):
        ref, _, _, send, recv = gathered[which]
        view = ref.at[h, slot_core, origin]
        return pltpu.make_async_remote_copy(
            src_ref=view, dst_ref=view, send_sem=send.at[h, k], recv_sem=recv.at[h, k],
            device_id={"exp_2": other}, device_id_type=MESH,
        )

    i, j = iota2(7 * block, UNIT * n)
    spread = ones_where(
        (j // UNIT == lax.rem(i, block) // 2)
        & (lax.rem(j, UNIT) == 2 * (i // block) + lax.rem(i, 2))
    )
    for h in range(2):
        pieces = jnp.dot(
            spread, xu[h].reshape(n * UNIT, quarter), preferred_element_type=F32
        ).astype(BF16)
        for g in range(2):
            xa[h, core, place[h], :, pl.ds(g * quarter, quarter)] = pieces[
                g * block : (g + 1) * block
            ]
        for g in range(4):
            xb[h, core, place[h], :, pl.ds(g * quarter, quarter)] = pieces[
                (g + 2) * block : (g + 3) * block
            ]
        xb[h, core, place[h], :, pl.ds(depth, wide - depth)] = pieces[
            6 * block : 7 * block, : wide - depth
        ]
    sent = []
    for which in range(2):
        for h in range(2):
            for d in range(2):
                copy = hop(which, h, d, 1, place[h])
                copy.start()
                sent.append(copy)
        for h in range(2):
            copy = share(which, h, core, place[h], 0)
            copy.start()
            sent.append(copy)
    for t in range(1, n // 2 + 1):
        for which in range(2):
            for h in range(2):
                for d in range(2):
                    origin = along(place[h], -t * (1 - 2 * d))
                    hop(which, h, d, t, origin).wait_recv()
                    if t < n // 2:
                        copy = hop(which, h, d, t + 1, origin)
                        copy.start()
                        sent.append(copy)
                        copy = share(which, h, core, origin, 2 * t - 1 + d)
                        copy.start()
                        sent.append(copy)
                    elif d == 1:
                        copy = share(which, h, core, origin, n - 1)
                        copy.start()
                        sent.append(copy)

    def arrivals(which):
        for h in range(2):
            for k in range(n):
                t = (k + 1) // 2
                origin = along(place[h], -t * (1 - 2 * ((k + 1) % 2)))
                share(which, h, other, origin, k).wait_recv()

    for copy in weights:
        copy.wait()

    arrivals(0)
    rows_a = 4 * n * n
    i, j = iota2(rows_a, rows_a)
    within = lax.rem(i, 2 * n * n)
    swap = ones_where(
        j == i - within + (lax.rem(within, block) // 2) * block + (within // block) * 2 + lax.rem(i, 2)
    )
    chunk = min(512, quarter)
    acc_a[...] = jnp.zeros_like(acc_a)

    def dense_in(k, carry):
        low = pl.ds(pl.multiple_of(k * chunk, chunk), chunk)
        high = pl.ds(pl.multiple_of(k * chunk + half, chunk), chunk)
        x0 = xa[0, :, :, :, low].reshape(rows_a, chunk)
        x1 = xa[1, :, :, :, low].reshape(rows_a, chunk)
        x1 = jnp.dot(swap, x1, preferred_element_type=F32).astype(BF16)
        for p, w in enumerate((wg, wu)):
            acc_a[p] += jnp.dot(x0, w[low, :], preferred_element_type=F32) + jnp.dot(
                x1, w[high, :], preferred_element_type=F32
            )
        return carry

    lax.fori_loop(0, half // chunk, dense_in, 0)
    hidden = (silu(acc_a[0]) * acc_a[1]).astype(BF16)
    hidden_swapped = jnp.dot(swap, hidden, preferred_element_type=F32).astype(BF16)

    def dense_out(k, carry):
        low = pl.ds(pl.multiple_of(k * chunk, chunk), chunk)
        high = pl.ds(pl.multiple_of(k * chunk + half, chunk), chunk)
        for h, (rows, columns) in enumerate(((hidden, low), (hidden_swapped, high))):
            oa[h, :, :, :, low] = (
                jnp.dot(rows, wd[:, columns], preferred_element_type=F32)
                .astype(BF16)
                .reshape(2, n, block, chunk)
            )
        return carry

    lax.fori_loop(0, half // chunk, dense_out, 0)

    arrivals(1)
    rows_b = 8 * n * n
    acc_b[...] = jnp.zeros_like(acc_b)

    def expert_in(k, carry):
        low = pl.ds(pl.multiple_of(k * chunk, chunk), chunk)
        x = xb[:, :, :, :, low].reshape(rows_b, chunk)
        acc_b[...] += jnp.dot(x, egu[low, :], preferred_element_type=F32)
        return carry

    lax.fori_loop(0, depth // chunk, expert_in, 0)
    units = egu.shape[1] // 2
    hidden = (silu(acc_b[:, :units]) * acc_b[:, units:]).astype(BF16)
    table = xb[:, :, :, :, pl.ds(depth, wide - depth)].reshape(rows_b, wide - depth).astype(F32)
    _, lane = iota2(rows_b, wide - depth)
    weight = jnp.sum(
        jnp.where((lane == expert) | (lane == expert + EXPERTS), table, 0.0), axis=1, keepdims=True
    )

    def expert_out(k, carry):
        low = pl.ds(pl.multiple_of(k * chunk, chunk), chunk)
        ob[:, :, :, :, low] = (
            (jnp.dot(hidden, ed[:, low], preferred_element_type=F32) * weight)
            .astype(BF16)
            .reshape(2, 2, n, block, chunk)
        )
        return carry

    lax.fori_loop(0, depth // chunk, expert_out, 0)

    reduced = ((oa, pa, ra, ta, qa, tpa, qpa), (ob, pb, rb, tb, qb, tpb, qpb))
    cut = ((pl.ds(0, quarter), pl.ds(quarter, quarter)), (pl.ds(0, half), pl.ds(half, half)))

    def give(which, h, k):
        ref, theirs, _, _, _, send, recv = reduced[which]
        return pltpu.make_async_remote_copy(
            src_ref=ref.at[h, other, along(place[h], n // 2 + k)],
            dst_ref=theirs.at[h, along(place[h], n // 2 + k)],
            send_sem=send.at[h, k], recv_sem=recv.at[h, k],
            device_id={"exp_2": other}, device_id_type=MESH,
        )

    def pass_on(which, h, d, t):
        ref, _, ring, send, recv = reduced[which][:5]
        slot = along(place[h], (n // 2 + 1 - t) * (1 - 2 * d))
        source, target = ref.at[h, core, slot], ring.at[h, d, t - 1]
        if t == 1:
            source = ref.at[h, core, slot, :, cut[which][d]]
            target = ring.at[h, d, 0, :, cut[which][d]]
        return pltpu.make_async_remote_copy(
            src_ref=source, dst_ref=target, send_sem=send.at[h, d, t - 1], recv_sem=recv.at[h, d, t - 1],
            device_id={LONG[h]: along(place[h], 1 - 2 * d)}, device_id_type=MESH,
        )

    def give_order():
        order = [0]
        for t in range(1, n // 2):
            order += [n - t, t]
        return order + [n // 2]

    for k in give_order():
        for which in range(2):
            for h in range(2):
                copy = give(which, h, k)
                copy.start()
                sent.append(copy)
    for t in range(1, n // 2 + 1):
        for which in range(2):
            ref, theirs, ring = reduced[which][:3]
            for h in range(2):
                if t == 1:
                    give(which, h, 0).wait_recv()
                for d in range(2):
                    sign = 1 - 2 * d
                    slot = along(place[h], (n // 2 + 1 - t) * sign)
                    if t == 1:
                        part = cut[which][d]
                        ref[h, core, slot, :, part] = (
                            ref[h, core, slot, :, part].astype(F32)
                            + theirs[h, slot, :, part].astype(F32)
                        ).astype(BF16)
                    else:
                        give(which, h, (n + (1 - t) * sign) % n).wait_recv()
                        pass_on(which, h, d, t - 1).wait_recv()
                        if t == 2:
                            for p in range(2):
                                part = cut[which][p]
                                total = ref[h, core, slot, :, part].astype(F32) + theirs[
                                    h, slot, :, part
                                ].astype(F32)
                                if p == d:
                                    total += ring[h, d, 0, :, part].astype(F32)
                                ref[h, core, slot, :, part] = total.astype(BF16)
                        else:
                            ref[h, core, slot] = (
                                ref[h, core, slot].astype(F32)
                                + theirs[h, slot].astype(F32)
                                + ring[h, d, t - 2].astype(F32)
                            ).astype(BF16)
                    copy = pass_on(which, h, d, t)
                    copy.start()
                    sent.append(copy)

    i, j = iota2(UNIT * n, 6 * block)
    collect = ones_where(
        (i // UNIT == lax.rem(j, block) // 2)
        & (lax.rem(i, UNIT) == 2 * (j // block) + lax.rem(j, 2))
    )
    last = []
    for h in range(2):
        totals = []
        for which in range(2):
            ref, theirs, ring = reduced[which][:3]
            give(which, h, n // 2).wait_recv()
            total = ref[h, core, place[h]].astype(F32) + theirs[h, place[h]].astype(F32)
            for d in range(2):
                pass_on(which, h, d, n // 2).wait_recv()
                total += ring[h, d, n // 2 - 1].astype(F32)
            totals.append(total.astype(BF16))
        stack = jnp.concatenate(
            [totals[0][:, g * quarter : (g + 1) * quarter] for g in range(2)]
            + [totals[1][:, g * quarter : (g + 1) * quarter] for g in range(4)],
            axis=0,
        )
        yu[h] = (
            jnp.dot(collect, stack, preferred_element_type=F32)
            .astype(BF16)
            .reshape(n, UNIT, quarter)
        )
        for k in sorted(range(1, n), key=lambda k: -min(k, n - k)):
            copy = pltpu.make_async_remote_copy(
                src_ref=yu.at[h, along(spot[h], k)], dst_ref=zu.at[h, k],
                send_sem=s2.at[h, k], recv_sem=r2.at[h, k],
                device_id={SHORT[h]: along(spot[h], k)}, device_id_type=MESH,
            )
            copy.start()
            last.append(copy)
    for copy in last:
        copy.wait_recv()
    for h in range(2):
        total = yu[h, spot[h]].astype(F32)
        for k in range(1, n):
            total += zu[h, k].astype(F32)
        out_ref[h] = total
    for copy in sent + last:
        copy.wait_send()


def layers(units, dense_gate, dense_up, dense_down, expert_gate, expert_up, expert_down):
    n = lax.axis_size("exp_0")
    depth, hidden = dense_gate.shape
    expert_hidden = expert_gate.shape[1]
    half, quarter, wide, block = depth // 2, depth // 4, depth + 128, 2 * n
    hops = n // 2
    dma = pltpu.SemaphoreType.DMA
    scratch = [
        pltpu.VMEM((2, n, UNIT, quarter), BF16),
        pltpu.VMEM((2, 2, n, block, half), BF16),
        pltpu.VMEM((2, 2, n, block, wide), BF16),
        pltpu.VMEM((depth, hidden), BF16),
        pltpu.VMEM((depth, hidden), BF16),
        pltpu.VMEM((hidden, depth), BF16),
        pltpu.VMEM((depth, 2 * expert_hidden), BF16),
        pltpu.VMEM((expert_hidden, depth), BF16),
        pltpu.VMEM((2, 4 * n * n, hidden), F32),
        pltpu.VMEM((8 * n * n, 2 * expert_hidden), F32),
        pltpu.VMEM((2, 2, n, block, half), BF16),
        pltpu.VMEM((2, 2, n, block, depth), BF16),
        pltpu.VMEM((2, n, block, half), BF16),
        pltpu.VMEM((2, n, block, depth), BF16),
        pltpu.VMEM((2, 2, hops, block, half), BF16),
        pltpu.VMEM((2, 2, hops, block, depth), BF16),
        pltpu.VMEM((2, n, UNIT, quarter), BF16),
        pltpu.VMEM((2, n, UNIT, quarter), BF16),
        dma((6,)),
        dma((2, n)), dma((2, n)),
        dma((2, 2, hops)), dma((2, 2, hops)), dma((2, 2, hops)), dma((2, 2, hops)),
        dma((2, n)), dma((2, n)), dma((2, n)), dma((2, n)),
        dma((2, 2, hops)), dma((2, 2, hops)), dma((2, 2, hops)), dma((2, 2, hops)),
        dma((2, n)), dma((2, n)), dma((2, n)), dma((2, n)),
        dma((2, n)), dma((2, n)),
    ]
    vmem = pl.BlockSpec(memory_space=pltpu.VMEM)
    anywhere = pl.BlockSpec(memory_space=pl.ANY)
    return pl.pallas_call(
        functools.partial(kernel, n),
        out_shape=jax.ShapeDtypeStruct((2, UNIT, quarter), F32),
        in_specs=[vmem] + [anywhere] * 6,
        out_specs=vmem,
        scratch_shapes=scratch,
        compiler_params=pltpu.CompilerParams(
            collective_id=0, has_side_effects=True, vmem_limit_bytes=64 * 1024 * 1024 - 65536
        ),
    )(units, dense_gate, dense_up, dense_down, expert_gate, expert_up, expert_down)


def normed(values, gain_vec):
    return values * lax.rsqrt(jnp.mean(values * values, axis=-1, keepdims=True) + 1e-06) * gain_vec


def shards(
    a_tokens,
    a_gain,
    dense_gate,
    dense_up,
    dense_down,
    b_tokens,
    b_gain,
    expert_ids,
    route_weights,
    expert_gate,
    expert_up,
    expert_down,
):
    depth = a_tokens.shape[1]
    quarter = depth // 4
    a_float = a_tokens.astype(F32)
    b_float = b_tokens.astype(F32)
    a_normed = normed(a_float, a_gain).astype(BF16)
    b_normed = normed(b_float, b_gain).astype(BF16)
    onehot = (expert_ids[:, :, None] == jnp.arange(EXPERTS, dtype=jnp.int32)).astype(F32)
    table = jnp.sum(route_weights[:, :, None] * onehot, axis=1)
    high = lax.reduce_precision(table, 8, 7)
    table = jnp.concatenate([high, table - high], axis=1).astype(BF16)
    table = jnp.pad(table, ((0, 0), (0, quarter - table.shape[1]))).reshape(2, 1, 2, quarter)
    a_unit = a_normed.reshape(2, 2, 2, quarter).transpose(1, 2, 0, 3)
    b_unit = b_normed.reshape(2, 2, 4, quarter).transpose(0, 2, 1, 3)
    empty = jnp.zeros((2, 1, 2, quarter), BF16)
    units = jnp.concatenate([a_unit, b_unit, table, empty], axis=1).reshape(2, UNIT, quarter)
    sums = layers(
        units, dense_gate, dense_up, dense_down, expert_gate[0], expert_up[0], expert_down[0]
    )
    sums = sums.reshape(2, UNIT // 2, 2, quarter)
    a_sum = sums[:, 0:2].transpose(2, 0, 1, 3).reshape(a_tokens.shape)
    b_sum = sums[:, 2:6].transpose(0, 2, 1, 3).reshape(b_tokens.shape)
    return ((a_float + a_sum).astype(BF16), (b_float + b_sum).astype(BF16))


def solution(mesh):
    finer = Mesh(
        mesh.devices.reshape(mesh.shape["rep"], 8, 8, 2), ("rep", "exp_0", "exp_1", "exp_2")
    )
    placed = (
        P(REP_EXP, None),
        P(),
        P(None, EXP),
        P(None, EXP),
        P(EXP, None),
        P(REP_EXP, None),
        P(),
        P(REP_EXP, None),
        P(REP_EXP, None),
        P(EXP, None, None),
        P(EXP, None, None),
        P(EXP, None, None),
    )
    return jax.shard_map(
        shards,
        mesh=finer,
        in_specs=placed,
        out_specs=(P(REP_EXP, None), P(REP_EXP, None)),
        check_vma=False,
    )
```

time: 558 us -> 141 us (0.25)
  waiting for transfers between devices: 374 us -> 0 us
  Pallas kernels: 0 us -> 122 us
  local copies, waits for them, and re-layouts: 63 us -> 9.7 us
  matrix products: 32.4 us -> 0 us
  blocking collectives: 24.3 us -> 0 us
  starting transfers between devices: 20.8 us -> 0 us
  other arithmetic: 23.6 us -> 7.63 us
  between operations: 14.2 us -> 0.71 us
    all_to_all x2 -> x0, waiting for transfers between devices: 171 us -> none  [the longest x1 152 us: shards(): lax.all_to_all(partial_value, EXP, split_axis=0, concat_axis=0, tiled=True)]
    ppermute x3 -> x0, waiting for transfers between devices: 140 us -> none  [from_partner(): lax.ppermute(array, axis, [(i, i ^ 1 << distance) for i in range(lax.axis...]
    pallas_call x0 -> x1, Pallas kernels: none -> 122 us  [layers(): pl.pallas_call(functools.partial(kernel, n), out_shape=jax.ShapeDtypeStru...]
    reduce_scatter x1 -> x0, waiting for transfers between devices: 63.3 us -> none  [scatter_lines(): own = lax.psum_scatter(lines, axis, scatter_dimension=0, tiled=True)]
    dot_general x7 -> x0, matrix products: 32.4 us -> none  [the longest x1 9.87 us: shards(): jnp.dot(block_rows, dense_down, preferred_element_type=jnp.float32)]
    all_to_all x1 -> x0, blocking collectives: 24.3 us -> none  [exchange_in_order(): lax.all_to_all(blocks, axes[k], split_axis=k, concat_axis=k, tiled=True)]
    reshape x2 -> x5, local copies, waits for them, and re-layouts: 20.6 us -> 1.85 us  [the longest x1 1.07 us: shards(): sums = sums.reshape(2, UNIT // 2, 2, quarter)]
    all_to_all x2 -> x0, starting transfers between devices: 16 us -> none  [the longest x1 9.54 us: shards(): lax.all_to_all(partial_value, EXP, split_axis=0, concat_axis=0, tiled=True)]
  transfers between devices with their start and end apart: 7 -> 0, of which waited for: 6 -> 0; matrix products, arithmetic and copies ran while one was open for 20% -> 0% of each run, Pallas kernels for 0% -> 0%
where the time goes in v1:
time: 141 us; the launch traced here: 140 us
  Pallas kernels  122 us (87%)
  local copies, waits for them, and re-layouts  9.7 us (7%)
  other arithmetic  7.63 us (5%)
    pallas_call x1, Pallas kernels, layers(): pl.pallas_call(functools.partial(kernel, n), out_shape=jax.ShapeDtypeStru...  122 us
    unnamed x5, local copies, waits for them, and re-layouts  7.73 us
    convert_element_type x2, other arithmetic, shards(): return ((a_float + a_sum).astype(BF16), (b_float + b_sum).astype(BF16))  2.86 us

profile of v1, /device:TPU:513, one launch (start us, length us, event | category | flops | bytes accessed | tf_op | source)
XLA Modules:
  0.0 140.0 jit_solution(13476804210704752779)
XLA Ops:
  0.6 0.9 fusion.4
  1.6 1.0 fusion
  2.6 0.1 pad.8.clone
  2.6 0.8 select_reduce_fusion
  3.4 0.1 fusion.10
  3.5 0.9 fusion.6
  4.4 0.9 fusion.2
  5.4 0.2 maximum_maximum_fusion
  5.6 0.7 reshape.48.u_ref
  6.3 0.0 copy-start
  6.3 4.7 %copy.23.wg_hbm = bf16[7168,144]{1,0:T(8,128)(2,1)} copy(bf16[7168,144]{0,1:T(8,128)(2,1)} %param.14) | data formatting | bytes 4128768 | tf_op args[2]
  11.0 0.0 copy-done
  11.0 2.9 %copy.24.wu_hbm = bf16[7168,144]{1,0:T(8,128)(2,1)} copy(bf16[7168,144]{0,1:T(8,128)(2,1)S(1)} %copy-done) | data formatting | bytes 4128768 | tf_op args[3]
  14.0 122.0 %shard_map.131 = f32[2,16,1792]{2,1,0:T(8,128)} custom-call(bf16[2,16,1792]{2,1,0:T(8,128)(2,1)} %reshape.48.u_ref, bf16[7168,144]{1,0:T(8,128)(2,1)} %copy.23.wg_hbm, bf16[7168,144]{1,0:T(8,128)(2,1)} %copy.24.wu_hbm, bf16[144,7168]{1,0:T(8,128)(2,1)} %wd_hbm.1, bf16[7168,128]{1,0:T(8,128)(2,1)} %bitcast.19, bf16[7168,128]{1,0:T(8,128)(2,1)} %bitcast.20, ...), custom_call_target="tpu_custom_call" | custom-call | tf_op jit(solution)/shard_map/pallas_call | solution.py:398
  135.9 1.1 reshape.49
  137.1 1.5 %fusion.3 = bf16[4,7168]{1,0:T(4,128)(2,1)} fusion(f32[4,7168]{1,0:T(4,128)S(1)} %bitcast.23, bf16[4,7168]{1,0:T(4,128)(2,1)} %param.17), kind=kLoop, calls=%fused_computation.6 | loop fusion | flops 86016 | bytes 229376 | tf_op jit(solution)/shard_map/convert_element_type | solution.py:449
  138.6 1.4 fusion.7
  (10 shorter events, 0.2 us)
Async XLA Ops:
  6.3 4.8 %copy-start = (bf16[7168,144]{0,1:T(8,128)(2,1)S(1)}, bf16[7168,144]{0,1:T(8,128)(2,1)}, u32[]{:S(2)}) copy-start(bf16[7168,144]{0,1:T(8,128)(2,1)} %param.15) | copy-start | bytes 6193156

commit v2 on v0

v2 whole, which is shorter than its diff:
```python
import functools

import jax
import jax.numpy as jnp
from jax import lax
from jax.experimental import pallas as pl
from jax.experimental.pallas import tpu as pltpu
from jax.sharding import Mesh
from jax.sharding import PartitionSpec as P

EXPERTS = 16
REP_EXP = ("rep", "exp_0", "exp_1", "exp_2")
EXP = ("exp_0", "exp_1", "exp_2")
LONG = ("exp_1", "exp_0")
SHORT = ("exp_0", "exp_1")
BF16 = jnp.bfloat16
F32 = jnp.float32
MESH = pl.DeviceIdType.MESH
UNIT = 16


def iota2(rows, columns):
    shape = (rows, columns)
    return lax.broadcasted_iota(jnp.int32, shape, 0), lax.broadcasted_iota(jnp.int32, shape, 1)


def ones_where(condition):
    return jnp.where(condition, 1.0, 0.0).astype(BF16)


def silu(values):
    return values / (1.0 + jnp.exp(-values))


def unit_place(i, n):
    j = i - 4 * n
    device = jnp.where(i < 4 * n, lax.rem(i, n), lax.rem(j, 2 * n) // 2)
    row = jnp.where(i < 4 * n, i // n, 4 + 2 * (j // (2 * n)) + lax.rem(j, 2))
    return device, row


def transposed_dot(rows, weight):
    return lax.dot_general(rows, weight, (((1,), (1,)), ((), ())), preferred_element_type=F32)


def kernel(
    n, a_ref, ag_ref, b_ref, bg_ref, ids_ref, route_ref,
    wg_hbm, wu_hbm, wd_hbm, eg_hbm, eu_hbm, ed_hbm, a_out, b_out,
    uf, u, xu, xa, xb, wg, wu, wd, egu, ed, acc_a, acc_b, oa, ob, pa, pb, ra, rb, yu, zu,
    a_sum, b_sum,
    w_sem, s1, r1, sa, ra_sem, sb, rb_sem, spa, rpa, spb, rpb,
    ta, qa, tb, qb, tpa, qpa, tpb, qpb, s2, r2,
):
    depth = a_ref.shape[1]
    half = depth // 2
    quarter = depth // 4
    wide = xb.shape[-1]
    last = n // 2
    core = lax.axis_index("exp_2")
    other = 1 - core
    place = [lax.axis_index(LONG[0]), lax.axis_index(LONG[1])]
    spot = [place[1], place[0]]
    expert = ((lax.axis_index("exp_0") * n + lax.axis_index("exp_1")) * 2 + core) // (
        2 * n * n // EXPERTS
    )

    def along(position, distance):
        return lax.rem(position + distance + n, n)

    barrier = pltpu.get_barrier_semaphore()
    pl.semaphore_signal(barrier, inc=1, device_id={"exp_2": other}, device_id_type=MESH)
    for h in range(2):
        for k in range(1, n):
            pl.semaphore_signal(
                barrier, inc=1, device_id={SHORT[h]: along(spot[h], k)}, device_id_type=MESH
            )

    units = eg_hbm.shape[1]
    weights = [
        pltpu.make_async_copy(wg_hbm, wg, w_sem.at[0]),
        pltpu.make_async_copy(wu_hbm, wu, w_sem.at[1]),
        pltpu.make_async_copy(wd_hbm, wd, w_sem.at[2]),
        pltpu.make_async_copy(eg_hbm, egu.at[:, pl.ds(0, units)], w_sem.at[3]),
        pltpu.make_async_copy(eu_hbm, egu.at[:, pl.ds(units, units)], w_sem.at[4]),
        pltpu.make_async_copy(ed_hbm, ed, w_sem.at[5]),
    ]
    for copy in weights:
        copy.start()

    a_float = a_ref[...].astype(F32)
    b_float = b_ref[...].astype(F32)
    a_normed = normed(a_float, ag_ref[...])
    b_normed = normed(b_float, bg_ref[...])
    uf[...] = jnp.zeros_like(uf)
    _, lane = iota2(b_ref.shape[0], wide - depth)
    table = jnp.zeros(lane.shape, F32)
    for k in range(ids_ref.shape[1]):
        hit = (lax.rem(lane, EXPERTS) == ids_ref[:, k : k + 1]) & (lane < 2 * EXPERTS)
        table += jnp.where(hit, route_ref[:, k : k + 1], 0.0)
    high = table.astype(BF16).astype(F32)
    table = jnp.where(lane < EXPERTS, high, table - high)
    for h in range(2):
        for g in range(4):
            part = slice(g * quarter, (g + 1) * quarter)
            uf[h, g : g + 1] = a_normed[h : h + 1, part]
            uf[h, 4 + 2 * g : 6 + 2 * g] = b_normed[2 * h : 2 * h + 2, part]
        uf[h, 12:14, 0 : wide - depth] = table[2 * h : 2 * h + 2]
    u[...] = uf[...].astype(BF16)

    pl.semaphore_wait(barrier, 2 * (n - 1) + 1)

    first = []
    for k in sorted(range(1, n), key=lambda k: -min(k, n - k)):
        for h in range(2):
            copy = pltpu.make_async_remote_copy(
                src_ref=u.at[h], dst_ref=xu.at[h, spot[h]],
                send_sem=s1.at[h, k], recv_sem=r1.at[h, k],
                device_id={SHORT[h]: along(spot[h], k)}, device_id_type=MESH,
            )
            copy.start()
            first.append(copy)
    for h in range(2):
        xu[h, spot[h]] = u[h]
    i, j = iota2(14 * n, UNIT * n)
    device, row = unit_place(i, n)
    spread = ones_where(j == device * UNIT + row)
    i, j = iota2(UNIT * n, 12 * n)
    device, row = unit_place(j, n)
    collect = ones_where(i == device * UNIT + row)
    for copy in first:
        copy.wait()

    gathered = ((xa, sa, ra_sem, spa, rpa), (xb, sb, rb_sem, spb, rpb))
    half_cut = ((pl.ds(0, half), pl.ds(half, half)),
                (pl.ds(0, half), pl.ds(half, wide - half)))
    sent = []

    def start(copy):
        copy.start()
        sent.append(copy)

    def hop(which, h, d, t, origin):
        ref, send, recv = gathered[which][:3]
        view = ref.at[h, core, origin]
        if t == last:
            view = ref.at[h, core, origin, :, half_cut[which][d]]
        return pltpu.make_async_remote_copy(
            src_ref=view, dst_ref=view, send_sem=send.at[h, d, t - 1], recv_sem=recv.at[h, d, t - 1],
            device_id={LONG[h]: along(place[h], 1 - 2 * d)}, device_id_type=MESH,
        )

    def share(which, h, slot_core, origin, k):
        ref, _, _, send, recv = gathered[which]
        view = ref.at[h, slot_core, origin]
        return pltpu.make_async_remote_copy(
            src_ref=view, dst_ref=view, send_sem=send.at[h, k], recv_sem=recv.at[h, k],
            device_id={"exp_2": other}, device_id_type=MESH,
        )

    for h in range(2):
        pieces = jnp.dot(
            spread, xu[h].reshape(n * UNIT, quarter), preferred_element_type=F32
        )
        for g in range(4):
            part = pl.ds(g * quarter, quarter)
            xa[h, core, place[h], :, part] = pieces[g * n : (g + 1) * n].astype(BF16)
            xb[h, core, place[h], :, part] = pieces[
                (4 + 2 * g) * n : (6 + 2 * g) * n
            ].astype(BF16)
        xb[h, core, place[h], :, pl.ds(depth, wide - depth)] = pieces[
            12 * n : 14 * n, : wide - depth
        ].astype(BF16)
    for which in range(2):
        for h in range(2):
            for d in range(2):
                start(hop(which, h, d, 1, place[h]))
        for h in range(2):
            start(share(which, h, core, place[h], 0))

    def steps(t):
        if t == 0:
            return [(h, 0, 0) for h in range(2)]
        if t == last:
            return [(h, last, n - 1) for h in range(2)]
        return [(h, t * (2 * d - 1), 2 * t - 1 + d) for h in range(2) for d in range(2)]

    def blocks_of(t):
        return [(h, c, along(place[h], s)) for h, s, _ in steps(t) for c in (core, other)]

    reduced = ((oa, pa, ra, ta, qa, tpa, qpa), (ob, pb, rb, tb, qb, tpb, qpb))
    cut = (pl.ds(0, half), pl.ds(half, half))

    def give(which, h, slot, k):
        ref, theirs, _, _, _, send, recv = reduced[which]
        return pltpu.make_async_remote_copy(
            src_ref=ref.at[h, other, slot], dst_ref=theirs.at[h, slot],
            send_sem=send.at[h, k], recv_sem=recv.at[h, k],
            device_id={"exp_2": other}, device_id_type=MESH,
        )

    chunk = min(1024, quarter)

    def layer(which, t):
        for h, s, k in steps(t):
            share(which, h, other, along(place[h], s), k).wait_recv()
        if t == 0:
            for copy in weights[3 * which : 3 * which + 3]:
                copy.wait()
        blocks = blocks_of(t)
        rows = (n, 2 * n)[which] * len(blocks)
        each = rows // len(blocks)

        def span(k):
            return pl.ds(pl.multiple_of(k * chunk, chunk), chunk)

        if which == 0:
            for p in range(2):
                acc_a[p, :rows] = jnp.zeros((rows, acc_a.shape[2]), F32)

            def dense_in(k, carry):
                x = jnp.concatenate(
                    [xa[h, c, slot, :, span(k)].astype(F32) for h, c, slot in blocks], axis=0
                ).astype(BF16)
                for p, w in enumerate((wg, wu)):
                    acc_a[p, :rows] += transposed_dot(x, w[:, span(k)])
                return carry

            lax.fori_loop(0, depth // chunk, dense_in, 0)
            hidden = (silu(acc_a[0, :rows]) * acc_a[1, :rows]).astype(BF16)

            def dense_out(k, carry):
                y = jnp.dot(hidden, wd[:, span(k)], preferred_element_type=F32)
                for i, (h, c, slot) in enumerate(blocks):
                    oa[h, c, slot, :, span(k)] = y[i * each : (i + 1) * each].astype(BF16)
                return carry

            lax.fori_loop(0, depth // chunk, dense_out, 0)
        else:
            acc_b[:rows] = jnp.zeros((rows, acc_b.shape[1]), F32)

            def expert_in(k, carry):
                x = jnp.concatenate([xb[h, c, slot, :, span(k)] for h, c, slot in blocks], axis=0)
                acc_b[:rows] += jnp.dot(x, egu[span(k), :], preferred_element_type=F32)
                return carry

            lax.fori_loop(0, depth // chunk, expert_in, 0)
            hidden = (silu(acc_b[:rows, :units]) * acc_b[:rows, units:]).astype(BF16)
            table = jnp.concatenate(
                [xb[h, c, slot, :, pl.ds(depth, wide - depth)] for h, c, slot in blocks], axis=0
            ).astype(F32)
            _, lane = iota2(rows, wide - depth)
            weight = jnp.sum(
                jnp.where((lane == expert) | (lane == expert + EXPERTS), table, 0.0),
                axis=1, keepdims=True,
            )

            def expert_out(k, carry):
                y = jnp.dot(hidden, ed[:, span(k)], preferred_element_type=F32) * weight
                for i, (h, c, slot) in enumerate(blocks):
                    ob[h, c, slot, :, span(k)] = y[i * each : (i + 1) * each].astype(BF16)
                return carry

            lax.fori_loop(0, depth // chunk, expert_out, 0)
        for h, s, k in steps(t):
            start(give(which, h, along(place[h], s), k))

    for t in range(1, last + 1):
        for which in range(2):
            layer(which, t - 1)
            for h in range(2):
                for d in range(2):
                    origin = along(place[h], -t * (1 - 2 * d))
                    hop(which, h, d, t, origin).wait_recv()
                    if t < last:
                        start(hop(which, h, d, t + 1, origin))
                        start(share(which, h, core, origin, 2 * t - 1 + d))
                    elif d == 1:
                        start(share(which, h, core, origin, n - 1))

    def pass_on(which, h, d, t):
        ref, _, ring, send, recv = reduced[which][:5]
        slot = along(place[h], (last + 1 - t) * (1 - 2 * d))
        source, target = ref.at[h, core, slot], ring.at[h, d, t - 1]
        if t == 1:
            source = ref.at[h, core, slot, :, cut[d]]
            target = ring.at[h, d, 0, :, cut[d]]
        return pltpu.make_async_remote_copy(
            src_ref=source, dst_ref=target, send_sem=send.at[h, d, t - 1], recv_sem=recv.at[h, d, t - 1],
            device_id={LONG[h]: along(place[h], 1 - 2 * d)}, device_id_type=MESH,
        )

    for t in range(1, last + 1):
        for which in range(2):
            ref, theirs, ring = reduced[which][:3]
            if t == 1:
                layer(which, last)
            for h in range(2):
                if t == 1:
                    give(which, h, along(place[h], last), n - 1).wait_recv()
                for d in range(2):
                    distance = last + 1 - t
                    slot = along(place[h], distance * (1 - 2 * d))
                    if t == 1:
                        ref[h, core, slot, :, cut[d]] = (
                            ref[h, core, slot, :, cut[d]].astype(F32)
                            + theirs[h, slot, :, cut[d]].astype(F32)
                        ).astype(BF16)
                    else:
                        give(which, h, slot, 2 * distance - d).wait_recv()
                        pass_on(which, h, d, t - 1).wait_recv()
                        for p in range(2):
                            total = ref[h, core, slot, :, cut[p]].astype(F32) + theirs[
                                h, slot, :, cut[p]
                            ].astype(F32)
                            if t > 2 or p == d:
                                total += ring[h, d, t - 2, :, cut[p]].astype(F32)
                            ref[h, core, slot, :, cut[p]] = total.astype(BF16)
                    start(pass_on(which, h, d, t))

    final = []
    for h in range(2):
        totals = []
        for which in range(2):
            ref, theirs, ring = reduced[which][:3]
            give(which, h, place[h], 0).wait_recv()
            total = ref[h, core, place[h]].astype(F32) + theirs[h, place[h]].astype(F32)
            for d in range(2):
                pass_on(which, h, d, last).wait_recv()
                total += ring[h, d, last - 1].astype(F32)
            totals += [total[:, g * quarter : (g + 1) * quarter] for g in range(4)]
        stack = jnp.concatenate(totals, axis=0).astype(BF16)
        yu[h] = (
            jnp.dot(collect, stack, preferred_element_type=F32)
            .astype(BF16)
            .reshape(n, UNIT, quarter)
        )
        for k in sorted(range(1, n), key=lambda k: -min(k, n - k)):
            copy = pltpu.make_async_remote_copy(
                src_ref=yu.at[h, along(spot[h], k)], dst_ref=zu.at[h, k],
                send_sem=s2.at[h, k], recv_sem=r2.at[h, k],
                device_id={SHORT[h]: along(spot[h], k)}, device_id_type=MESH,
            )
            start(copy)
            final.append(copy)
    for copy in final:
        copy.wait_recv()
    for h in range(2):
        total = yu[h, spot[h]].astype(F32)
        for k in range(1, n):
            total += zu[h, k].astype(F32)
        uf[h] = total
    for h in range(2):
        for g in range(4):
            part = pl.ds(g * quarter, quarter)
            a_sum[h : h + 1, part] = uf[h, g : g + 1]
            b_sum[2 * h : 2 * h + 2, part] = uf[h, 4 + 2 * g : 6 + 2 * g]
    a_out[...] = (a_ref[...].astype(F32) + a_sum[...]).astype(BF16)
    b_out[...] = (b_ref[...].astype(F32) + b_sum[...]).astype(BF16)
    for copy in sent:
        copy.wait_send()


def normed(values, gain_vec):
    return values * lax.rsqrt(jnp.mean(values * values, axis=-1, keepdims=True) + 1e-06) * gain_vec


def shards(
    a_tokens,
    a_gain,
    dense_gate,
    dense_up,
    dense_down,
    b_tokens,
    b_gain,
    expert_ids,
    route_weights,
    expert_gate,
    expert_up,
    expert_down,
):
    n = lax.axis_size("exp_0")
    depth, hidden = dense_gate.shape
    units = expert_gate.shape[2]
    quarter, wide = depth // 4, depth + 128
    hops = n // 2
    dma = pltpu.SemaphoreType.DMA
    scratch = [
        pltpu.VMEM((2, UNIT, quarter), F32),
        pltpu.VMEM((2, UNIT, quarter), BF16),
        pltpu.VMEM((2, n, UNIT, quarter), BF16),
        pltpu.VMEM((2, 2, n, n, depth), BF16),
        pltpu.VMEM((2, 2, n, 2 * n, wide), BF16),
        pltpu.VMEM((hidden, depth), BF16),
        pltpu.VMEM((hidden, depth), BF16),
        pltpu.VMEM((hidden, depth), BF16),
        pltpu.VMEM((depth, 2 * units), BF16),
        pltpu.VMEM((units, depth), BF16),
        pltpu.VMEM((2, 8 * n, hidden), F32),
        pltpu.VMEM((16 * n, 2 * units), F32),
        pltpu.VMEM((2, 2, n, n, depth), BF16),
        pltpu.VMEM((2, 2, n, 2 * n, depth), BF16),
        pltpu.VMEM((2, n, n, depth), BF16),
        pltpu.VMEM((2, n, 2 * n, depth), BF16),
        pltpu.VMEM((2, 2, hops, n, depth), BF16),
        pltpu.VMEM((2, 2, hops, 2 * n, depth), BF16),
        pltpu.VMEM((2, n, UNIT, quarter), BF16),
        pltpu.VMEM((2, n, UNIT, quarter), BF16),
        pltpu.VMEM(a_tokens.shape, F32),
        pltpu.VMEM(b_tokens.shape, F32),
        dma((6,)),
        dma((2, n)), dma((2, n)),
        dma((2, 2, hops)), dma((2, 2, hops)), dma((2, 2, hops)), dma((2, 2, hops)),
        dma((2, n)), dma((2, n)), dma((2, n)), dma((2, n)),
        dma((2, 2, hops)), dma((2, 2, hops)), dma((2, 2, hops)), dma((2, 2, hops)),
        dma((2, n)), dma((2, n)), dma((2, n)), dma((2, n)),
        dma((2, n)), dma((2, n)),
    ]
    vmem = pl.BlockSpec(memory_space=pltpu.VMEM)
    anywhere = pl.BlockSpec(memory_space=pl.ANY)
    return pl.pallas_call(
        functools.partial(kernel, n),
        out_shape=(
            jax.ShapeDtypeStruct(a_tokens.shape, BF16),
            jax.ShapeDtypeStruct(b_tokens.shape, BF16),
        ),
        in_specs=[vmem] * 6 + [anywhere] * 6,
        out_specs=(vmem, vmem),
        scratch_shapes=scratch,
        compiler_params=pltpu.CompilerParams(
            collective_id=0, has_side_effects=True, vmem_limit_bytes=64 * 1024 * 1024 - 65536
        ),
    )(
        a_tokens,
        a_gain[None, :],
        b_tokens,
        b_gain[None, :],
        expert_ids,
        route_weights,
        dense_gate.T,
        dense_up.T,
        dense_down,
        expert_gate[0],
        expert_up[0],
        expert_down[0],
    )


def solution(mesh):
    finer = Mesh(
        mesh.devices.reshape(mesh.shape["rep"], 8, 8, 2), ("rep", "exp_0", "exp_1", "exp_2")
    )
    placed = (
        P(REP_EXP, None),
        P(),
        P(None, EXP),
        P(None, EXP),
        P(EXP, None),
        P(REP_EXP, None),
        P(),
        P(REP_EXP, None),
        P(REP_EXP, None),
        P(EXP, None, None),
        P(EXP, None, None),
        P(EXP, None, None),
    )
    return jax.shard_map(
        shards,
        mesh=finer,
        in_specs=placed,
        out_specs=(P(REP_EXP, None), P(REP_EXP, None)),
        check_vma=False,
    )
```

time: 558 us -> 119 us (0.21)
  waiting for transfers between devices: 374 us -> 0 us
  Pallas kernels: 0 us -> 115 us
  local copies, waits for them, and re-layouts: 63 us -> 2.84 us
  matrix products: 32.4 us -> 0 us
  blocking collectives: 24.3 us -> 0 us
  other arithmetic: 23.6 us -> 0 us
  starting transfers between devices: 20.8 us -> 0 us
  between operations: 14.2 us -> 0.64 us
    all_to_all x2 -> x0, waiting for transfers between devices: 171 us -> none  [the longest x1 152 us: shards(): lax.all_to_all(partial_value, EXP, split_axis=0, concat_axis=0, tiled=True)]
    ppermute x3 -> x0, waiting for transfers between devices: 140 us -> none  [from_partner(): lax.ppermute(array, axis, [(i, i ^ 1 << distance) for i in range(lax.axis...]
    pallas_call x0 -> x1, Pallas kernels: none -> 115 us  [shards(): pl.pallas_call(functools.partial(kernel, n), out_shape=(jax.ShapeDtypeStr...]
    reduce_scatter x1 -> x0, waiting for transfers between devices: 63.3 us -> none  [scatter_lines(): own = lax.psum_scatter(lines, axis, scatter_dimension=0, tiled=True)]
    dot_general x7 -> x0, matrix products: 32.4 us -> none  [the longest x1 9.87 us: shards(): jnp.dot(block_rows, dense_down, preferred_element_type=jnp.float32)]
    all_to_all x1 -> x0, blocking collectives: 24.3 us -> none  [exchange_in_order(): lax.all_to_all(blocks, axes[k], split_axis=k, concat_axis=k, tiled=True)]
    reshape x2 -> x0, local copies, waits for them, and re-layouts: 20.6 us -> none  [the longest x1 12.3 us: shards(): partial_value = partial_value.reshape(sources, item_count, model_width)]
    all_to_all x2 -> x0, starting transfers between devices: 16 us -> none  [the longest x1 9.54 us: shards(): lax.all_to_all(partial_value, EXP, split_axis=0, concat_axis=0, tiled=True)]
  transfers between devices with their start and end apart: 7 -> 0, of which waited for: 6 -> 0; matrix products, arithmetic and copies ran while one was open for 20% -> 0% of each run, Pallas kernels for 0% -> 0%
where the time goes in v2:
time: 119 us; the launch traced here: 118 us
  Pallas kernels  115 us (97%)
  local copies, waits for them, and re-layouts  2.84 us (2%)
    pallas_call x1, Pallas kernels, shards(): pl.pallas_call(functools.partial(kernel, n), out_shape=(jax.ShapeDtypeStr...  115 us
    unnamed x2, local copies, waits for them, and re-layouts  2.84 us

profile of v2, /device:TPU:513, one launch (start us, length us, event | category | flops | bytes accessed | tf_op | source)
XLA Modules:
  0.0 118.5 jit_solution(15209663143517571006)
XLA Ops:
  0.6 115.0 %shard_map.131 = (bf16[2,7168]{1,0:T(2,128)(2,1)}, bf16[4,7168]{1,0:T(4,128)(2,1)}) custom-call(bf16[2,7168]{1,0:T(2,128)(2,1)} %a_ref.1, f32[1,7168]{1,0:T(1,128)} %bitcast.12, bf16[4,7168]{1,0:T(4,128)(2,1)} %b_ref.1, f32[1,7168]{1,0:T(1,128)} %bitcast.13, s32[4,8]{1,0:T(4,128)} %ids_ref.1, f32[4,8]{1,0:T(4,128)} %route_ref.1, bf16[144,7168]{1,0:T(8,128)(2,1)} %bitcast.7, ...), custom_call_target="tpu_custom_call" | custom-call | tf_op jit(solution)/shard_map/pallas_call | solution.py:420
  115.6 1.4 %copy.16 = bf16[2,7168]{1,0:T(2,128)(2,1)} copy(bf16[2,7168]{1,0:T(2,128)(2,1)} %get-tuple-element.4) | data formatting | bytes 57344
  117.0 1.5 %copy.17 = bf16[4,7168]{1,0:T(4,128)(2,1)} copy(bf16[4,7168]{1,0:T(4,128)(2,1)} %get-tuple-element.5) | data formatting | bytes 114688
